TPU v7x, 32 devices: a whole 2x2x4 slice. The times are simulated.
32 devices in a mesh: expert: 2 (over x), batch: 4 (over z), seq: 4 (over y, core).
Axes of the slice: x: 2, y: 2, z: 4, core: 2. Of those that a mesh axis runs over, the one named last changes fastest.
Arguments:
- queries: bfloat16 [2, 4, 2, 384, 4096], P('expert', 'batch', None, 'seq'), may hold values from -36 to 36
- keys: bfloat16 [2, 4, 2, 384, 4096], P('expert', 'batch', None, 'seq'), may hold values from -21 to 21
- values: bfloat16 [2, 4, 2, 384, 4096], P('expert', 'batch', None, 'seq'), may hold values from -6 to 6
- latents: bfloat16 [2, 4, 384, 4096], P('expert', 'batch', 'seq'), may hold values from -6 to 6
- gain: bfloat16 [2, 4096], P('expert'), may hold values from 0.099609375 to 1.8984375
- steps_table: int32 [2, 4], P('expert', 'batch'), may hold values from 0 to 38
- flags: int32 [4], P('batch'), may hold values 0 or 1
Outputs:
- denoised: bfloat16 [2, 4, 384, 4096], P('expert', 'batch', 'seq')
- next_latents: bfloat16 [2, 4, 384, 4096], P('expert', 'batch', 'seq')
All inputs are finite; a program needn't handle non-finite values. No bound on the sum of `flags` on one device may be relied on, other than what follows from the above.
Results may differ from a plain program's by a relative error of at most 0.006.
Values may be sent and summed in bfloat16 or wider, within the bound.
A program may use at most 64 MiB of HBM per device.

v0:
```python
import jax
import jax.numpy as jnp
from jax import lax
from jax.sharding import PartitionSpec as P

HDIM = 128
STEPS = 40
GUIDANCE = 3.5
flow_shift = 5.0


def from_partner(block, axis, bit):
    count = lax.axis_size(axis)
    route = []
    for low in range(count):
        high = low | 1 << bit
        if high != low and high < count:
            route += [(low, high), (high, low)]
    return lax.ppermute(block, axis, route)


def sigma_of(step):
    level = 1.0 - step.astype(jnp.float32) / STEPS
    return flow_shift * level / (1.0 + (flow_shift - 1.0) * level)


def combine(cond, uncond):
    base = uncond.astype(jnp.float32)
    return (base + GUIDANCE * (cond.astype(jnp.float32) - base)).astype(jnp.bfloat16)


def attend(stacked):
    query_heads, key_heads, value_heads = stacked
    items, length, width_dev = query_heads.shape
    heads_dev = width_dev // HDIM
    block = 512 if length % 512 == 0 else length
    key_rows = key_heads.reshape(items, length, heads_dev, HDIM)
    value_rows = value_heads.reshape(items, length, heads_dev, HDIM)
    query_blocks = query_heads.reshape(items, length // block, block, heads_dev, HDIM).transpose(
        1, 0, 2, 3, 4
    )

    def one_block(query_part):
        scores = jnp.einsum(
            "nqhd,nkhd->nhqk", query_part, key_rows, preferred_element_type=jnp.float32
        ) * HDIM ** (-0.5)
        weights = jax.nn.softmax(scores, axis=-1).astype(jnp.bfloat16)
        return jnp.einsum(
            "nhqk,nkhd->nqhd", weights, value_rows, preferred_element_type=jnp.float32
        ).astype(jnp.bfloat16)

    result = lax.map(one_block, query_blocks)
    return result.transpose(1, 0, 2, 3, 4).reshape(items, length, width_dev)


def per_device(queries, keys, values, latents, gain, steps_table, flags):
    attended = attend(
        (
            lax.all_to_all(queries[0, 0], "seq", split_axis=2, concat_axis=1, tiled=True),
            lax.all_to_all(keys[0, 0], "seq", split_axis=2, concat_axis=1, tiled=True),
            lax.all_to_all(values[0, 0], "seq", split_axis=2, concat_axis=1, tiled=True),
        )
    )
    guided = lax.all_to_all(
        combine(attended[0], attended[1]), "seq", split_axis=0, concat_axis=1, tiled=True
    )
    guided_f32 = guided.astype(jnp.float32)
    scale = lax.rsqrt(jnp.mean(guided_f32 * guided_f32, axis=-1, keepdims=True) + 1e-06)
    velocity = guided_f32 * scale * gain[0].astype(jnp.float32)[None, :]
    step_now = steps_table[0, 0]
    sigma_now = sigma_of(step_now)
    sigma_next = sigma_of(step_now + 1)
    current = latents[0, 0].astype(jnp.float32)
    denoised = (current - sigma_now * velocity).astype(jnp.bfloat16)
    moved = (current + (sigma_next - sigma_now) * velocity).astype(jnp.bfloat16)
    partner = from_partner(moved, "expert", 0)
    next_latents = jnp.where(flags[0] == 1, partner, moved)
    return (denoised[None, None], next_latents[None, None])


def solution(mesh):
    placed = (
        P("expert", "batch", None, "seq", None),
        P("expert", "batch", None, "seq", None),
        P("expert", "batch", None, "seq", None),
        P("expert", "batch", "seq", None),
        P("expert", None),
        P("expert", "batch"),
        P("batch"),
    )
    return jax.shard_map(
        per_device,
        mesh=mesh,
        in_specs=placed,
        out_specs=(P("expert", "batch", "seq", None), P("expert", "batch", "seq", None)),
        check_vma=False,
    )
```

profile of v0, /device:TPU:0, one launch (start us, length us, event | category | flops | bytes accessed | tf_op | source)
XLA Modules:
  0.0 159.6 jit_solution(14842761862056379476)
XLA Ops:
  0.6 5.7 %copy.30 = bf16[1,1,2,96,4096]{3,2,4,1,0:T(2,128)(2,1)} copy(bf16[1,1,2,96,4096]{4,3,2,1,0:T(8,128)(2,1)} %param.7) | data formatting | bytes 3145728 | tf_op args[0]
  6.3 4.3 %all-to-all-start = ((bf16[2,96,4096]{1,0,2:T(2,128)(2,1)}), bf16[2,96,4096]{1,0,2:T(2,128)(2,1)S(1)}, u32[]{:S(2)}, u32[]{:S(2)}) async-start(bf16[2,96,4096]{1,0,2:T(2,128)(2,1)} %bitcast.50), calls=%async_computation | async-start | bytes 4194304 | tf_op jit(solution)/shard_map/all_to_all | solution.py:59
  10.6 5.7 %copy.32 = bf16[1,1,2,96,4096]{3,2,4,1,0:T(2,128)(2,1)} copy(bf16[1,1,2,96,4096]{4,3,2,1,0:T(8,128)(2,1)} %param.8) | data formatting | bytes 3145728 | tf_op args[1]
  16.3 20.0 %all-to-all-done = bf16[2,96,4096]{1,0,2:T(2,128)(2,1)S(1)} async-done(((bf16[2,96,4096]{1,0,2:T(2,128)(2,1)}), bf16[2,96,4096]{1,0,2:T(2,128)(2,1)S(1)}, u32[]{:S(2)}, u32[]{:S(2)}) %all-to-all-start) | async-done | bytes 1572896 | tf_op jit(solution)/shard_map/all_to_all | solution.py:59
  36.3 4.4 %all-to-all-start.1 = ((bf16[2,96,4096]{1,0,2:T(2,128)(2,1)}), bf16[2,96,4096]{1,0,2:T(2,128)(2,1)}, u32[]{:S(2)}, u32[]{:S(2)}) async-start(bf16[2,96,4096]{1,0,2:T(2,128)(2,1)} %bitcast.49), calls=%async_computation.1 | async-start | bytes 4194304 | tf_op jit(solution)/shard_map/all_to_all | solution.py:60
  40.7 5.7 %copy.36 = bf16[1,1,2,96,4096]{3,2,4,1,0:T(2,128)(2,1)} copy(bf16[1,1,2,96,4096]{4,3,2,1,0:T(8,128)(2,1)} %param.9) | data formatting | bytes 3145728 | tf_op args[2]
  46.4 20.0 %all-to-all-done.1 = bf16[2,96,4096]{1,0,2:T(2,128)(2,1)} async-done(((bf16[2,96,4096]{1,0,2:T(2,128)(2,1)}), bf16[2,96,4096]{1,0,2:T(2,128)(2,1)}, u32[]{:S(2)}, u32[]{:S(2)}) %all-to-all-start.1) | async-done | bytes 1572896 | tf_op jit(solution)/shard_map/all_to_all | solution.py:60
  66.4 4.4 %all-to-all-start.2 = ((bf16[2,96,4096]{1,0,2:T(2,128)(2,1)}), bf16[2,96,4096]{1,0,2:T(2,128)(2,1)}, u32[]{:S(2)}, u32[]{:S(2)}) async-start(bf16[2,96,4096]{1,0,2:T(2,128)(2,1)} %bitcast.48), calls=%async_computation.2 | async-start | bytes 4194304 | tf_op jit(solution)/shard_map/all_to_all | solution.py:61
  70.9 3.7 %copy.31 = bf16[2,96,4,1024]{3,1,2,0:T(8,128)(2,1)} copy(bf16[2,96,4,1024]{1,0,3,2:T(2,128)(2,1)S(1)} %bitcast.47) | data formatting | bytes 3145728 | tf_op jit(solution)/shard_map/all_to_all | solution.py:59
  74.6 1.8 %copy.46 = bf16[96,8,8,128]{3,2,1,0:T(8,128)(2,1)S(1)} copy(bf16[96,8,8,128]{3,1,2,0:T(8,128)(2,1)} %bitcast.54) | data formatting | bytes 3145728
  76.4 4.7 %copy.33 = bf16[2,96,4,1024]{3,1,2,0:T(8,128)(2,1)S(1)} copy(bf16[2,96,4,1024]{1,0,3,2:T(2,128)(2,1)} %bitcast.5) | data formatting | bytes 3145728 | tf_op jit(solution)/shard_map/all_to_all | solution.py:60
  83.0 3.6 %copy-done = f32[2,8,384,384]{2,3,1,0:T(8,128)} copy-done((f32[2,8,384,384]{2,3,1,0:T(8,128)}, f32[2,8,384,384]{2,3,1,0:T(8,128)S(1)}, u32[]{:S(2)}) %copy-start) | copy-done | bytes 9437208
  86.6 2.4 %fusion.26 = f32[2,8,384]{2,1,0:T(8,128)S(1)} fusion(f32[2,8,384,384]{2,3,1,0:T(8,128)S(1)} %fusion.12), kind=kOutput, calls=%fused_computation.30 | output fusion | flops 9437567 | bytes 9461760 | tf_op jit(solution)/shard_map/while/body/eval_jaxpr/sub | solution.py:47
  89.0 7.6 %all-to-all-done.2 = bf16[2,96,4096]{1,0,2:T(2,128)(2,1)} async-done(((bf16[2,96,4096]{1,0,2:T(2,128)(2,1)}), bf16[2,96,4096]{1,0,2:T(2,128)(2,1)}, u32[]{:S(2)}, u32[]{:S(2)}) %all-to-all-start.2) | async-done | bytes 1572896 | tf_op jit(solution)/shard_map/all_to_all | solution.py:61
  96.6 4.7 %copy.37 = bf16[2,96,4,1024]{3,1,2,0:T(8,128)(2,1)S(1)} copy(bf16[2,96,4,1024]{1,0,3,2:T(2,128)(2,1)} %bitcast.8) | data formatting | bytes 3145728 | tf_op jit(solution)/shard_map/all_to_all | solution.py:61
  101.7 9.9 %fusion.15 = bf16[2,384,8,128]{3,1,2,0:T(8,128)(2,1)S(1)} fusion(bf16[2,384,8,128]{3,2,1,0:T(8,128)(2,1)S(1)} %bitcast.57, f32[2,8,384]{2,1,0:T(8,128)S(1)} %fusion.26, f32[2,8,384,384]{2,3,1,0:T(8,128)} %copy-done), kind=kOutput, calls=%fused_computation.22 | convolution fusion | flops 616569216 | bytes 12607488 | tf_op jit(solution)/shard_map/while/body/eval_jaxpr/nhqk,nkhd->nqhd/dot_general | solution.py:48
  112.8 1.4 reshape.129
  117.0 2.6 %add_convert_fusion = bf16[4,96,1024]{2,1,0:T(8,128)(2,1)} fusion(f32[4,96,1024]{2,1,0:T(8,128)S(1)} %copy-done.1, f32[4,96,1024]{2,1,0:T(8,128)} %reshape.130), kind=kLoop, calls=%fused_computation.21 | loop fusion | flops 1572864 | bytes 3932160 | tf_op jit(solution)/shard_map/convert_element_type | solution.py:29
  119.7 3.8 %all-to-all-start.3 = ((bf16[4,96,1024]{2,1,0:T(8,128)(2,1)}), bf16[4,96,1024]{2,1,0:T(8,128)(2,1)S(1)}, u32[]{:S(2)}, u32[]{:S(2)}) async-start(bf16[4,96,1024]{2,1,0:T(8,128)(2,1)} %add_convert_fusion), calls=%async_computation.3 | async-start | bytes 1572864 | tf_op jit(solution)/shard_map/all_to_all | solution.py:64
  124.9 10.0 %all-to-all-done.3 = bf16[4,96,1024]{2,1,0:T(8,128)(2,1)S(1)} async-done(((bf16[4,96,1024]{2,1,0:T(8,128)(2,1)}), bf16[4,96,1024]{2,1,0:T(8,128)(2,1)S(1)}, u32[]{:S(2)}, u32[]{:S(2)}) %all-to-all-start.3) | async-done | bytes 786464 | tf_op jit(solution)/shard_map/all_to_all | solution.py:64
  137.7 2.3 %collective-permute-start = (bf16[96,4096]{1,0:T(8,128)(2,1)}, bf16[96,4096]{1,0:T(8,128)(2,1)}, u32[]{:S(2)}, u32[]{:S(2)}) collective-permute-start(bf16[96,4096]{1,0:T(8,128)(2,1)} %fusion.9), channel_id=1, source_target_pairs={{0,16},{16,0},{1,17},{17,1},{2,18},{18,2},{3,19},{19,3},{4,20},{20... | collective-permute-start | bytes 2359304 | tf_op jit(solution)/shard_map/ppermute | solution.py:19
  142.0 2.4 %fusion.7 = bf16[1,1,96,4096]{3,2,1,0:T(8,128)(2,1)} fusion(bf16[1,1,96,4096]{3,2,1,0:T(8,128)(2,1)} %param.10, f32[1,1,96,4096]{3,2,1,0:T(8,128)S(1)} %reshape.131, f32[4096]{0:T(1024)S(1)} %bitcast.59, f32[96]{0:T(128)S(1)} %add_rsqrt_fusion, f32[]{:T(128)} %bitcast), kind=kLoop, calls=%fused_computation.13 | loop fusion | flops 2359296 | bytes 3162500 | tf_op jit(solution)/shard_map/convert_element_type | solution.py:74
  144.4 13.1 %collective-permute-done = bf16[96,4096]{1,0:T(8,128)(2,1)} collective-permute-done((bf16[96,4096]{1,0:T(8,128)(2,1)}, bf16[96,4096]{1,0:T(8,128)(2,1)}, u32[]{:S(2)}, u32[]{:S(2)}) %collective-permute-start) | collective-permute-done | bytes 786464 | tf_op jit(solution)/shard_map/ppermute | solution.py:19
  157.5 2.1 %select_bitcast_fusion = bf16[1,1,96,4096]{3,2,1,0:T(8,128)(2,1)} fusion(bf16[96,4096]{1,0:T(8,128)(2,1)} %collective-permute-done, bf16[96,4096]{1,0:T(8,128)(2,1)} %fusion.9, pred[]{:T(512)} %bitcast.13), kind=kLoop, calls=%fused_computation.25 | loop fusion | flops 393216 | bytes 2359297 | tf_op jit(solution)/shard_map/broadcast_in_dim | solution.py:78
  (22 shorter events, 11.1 us)
Async XLA Ops:
  6.3 29.9 %all-to-all-start = ((bf16[2,96,4096]{1,0,2:T(2,128)(2,1)}), bf16[2,96,4096]{1,0,2:T(2,128)(2,1)S(1)}, u32[]{:S(2)}, u32[]{:S(2)}) async-start(bf16[2,96,4096]{1,0,2:T(2,128)(2,1)} %bitcast.50), calls=%async_computation | async-start | bytes 4194304 | tf_op jit(solution)/shard_map/all_to_all | solution.py:59
  36.3 30.2 %all-to-all-start.1 = ((bf16[2,96,4096]{1,0,2:T(2,128)(2,1)}), bf16[2,96,4096]{1,0,2:T(2,128)(2,1)}, u32[]{:S(2)}, u32[]{:S(2)}) async-start(bf16[2,96,4096]{1,0,2:T(2,128)(2,1)} %bitcast.49), calls=%async_computation.1 | async-start | bytes 4194304 | tf_op jit(solution)/shard_map/all_to_all | solution.py:60
  66.4 30.2 %all-to-all-start.2 = ((bf16[2,96,4096]{1,0,2:T(2,128)(2,1)}), bf16[2,96,4096]{1,0,2:T(2,128)(2,1)}, u32[]{:S(2)}, u32[]{:S(2)}) async-start(bf16[2,96,4096]{1,0,2:T(2,128)(2,1)} %bitcast.48), calls=%async_computation.2 | async-start | bytes 4194304 | tf_op jit(solution)/shard_map/all_to_all | solution.py:61
  83.0 3.6 %copy-start = (f32[2,8,384,384]{2,3,1,0:T(8,128)}, f32[2,8,384,384]{2,3,1,0:T(8,128)S(1)}, u32[]{:S(2)}) copy-start(f32[2,8,384,384]{2,3,1,0:T(8,128)S(1)} %fusion.12) | copy-start | bytes 28311556
  115.1 1.9 %copy-start.1 = (f32[4,96,1024]{2,1,0:T(8,128)S(1)}, f32[4,96,1024]{2,1,0:T(8,128)}, u32[]{:S(2)}) copy-start(f32[4,96,1024]{2,1,0:T(8,128)} %reshape.129) | copy-start | bytes 4718596
  119.7 4.5 %copy-start.3 = (bf16[1,4096]{1,0:T(2,128)(2,1)S(1)}, bf16[1,4096]{1,0:T(2,128)(2,1)}, u32[]{:S(2)}) copy-start(bf16[1,4096]{1,0:T(2,128)(2,1)} %param.11) | copy-start | bytes 24580
  119.7 15.2 %all-to-all-start.3 = ((bf16[4,96,1024]{2,1,0:T(8,128)(2,1)}), bf16[4,96,1024]{2,1,0:T(8,128)(2,1)S(1)}, u32[]{:S(2)}, u32[]{:S(2)}) async-start(bf16[4,96,1024]{2,1,0:T(8,128)(2,1)} %add_convert_fusion), calls=%async_computation.3 | async-start | bytes 1572864 | tf_op jit(solution)/shard_map/all_to_all | solution.py:64
  135.3 1.1 copy-start.2
  137.7 19.8 %collective-permute-start = (bf16[96,4096]{1,0:T(8,128)(2,1)}, bf16[96,4096]{1,0:T(8,128)(2,1)}, u32[]{:S(2)}, u32[]{:S(2)}) collective-permute-start(bf16[96,4096]{1,0:T(8,128)(2,1)} %fusion.9), channel_id=1, source_target_pairs={{0,16},{16,0},{1,17},{17,1},{2,18},{18,2},{3,19},{19,3},{4,20},{20... | collective-permute-start | bytes 2359304 | tf_op jit(solution)/shard_map/ppermute | solution.py:19
where the time goes:
time: 161 us; the launch traced here: 160 us
  waiting for transfers between devices  70.7 us (44%)
  local copies, waits for them, and re-layouts  44.6 us (28%)
  starting transfers between devices  19.2 us (12%)
  other arithmetic  11.6 us (7%)
  matrix products  11.3 us (7%)
  between operations  2.2 us (1%)
    unnamed x14, local copies, waits for them, and re-layouts  24.7 us
    all_to_all x1, waiting for transfers between devices, per_device(): lax.all_to_all(keys[0, 0], 'seq', split_axis=2, concat_axis=1, tiled=True)  20 us
    all_to_all x1, waiting for transfers between devices, per_device(): lax.all_to_all(queries[0, 0], 'seq', split_axis=2, concat_axis=1, tiled=T...  20 us
    ppermute x1, waiting for transfers between devices, from_partner(): return lax.ppermute(block, axis, route)  13.1 us
    all_to_all x1, waiting for transfers between devices, per_device(): lax.all_to_all(combine(attended[0], attended[1]), 'seq', split_axis=0, co...  9.97 us
    dot_general x1, matrix products, one_block(): jnp.einsum('nhqk,nkhd->nqhd', weights, value_rows, preferred_element_type...  9.9 us
    all_to_all x1, waiting for transfers between devices, per_device(): lax.all_to_all(values[0, 0], 'seq', split_axis=2, concat_axis=1, tiled=True)  7.6 us
    all_to_all x1, local copies, waits for them, and re-layouts, per_device(): lax.all_to_all(keys[0, 0], 'seq', split_axis=2, concat_axis=1, tiled=True)  4.67 us
  transfers between devices with their start and end apart: 5, of which 5 were waited for; matrix products, arithmetic and copies ran while one was open for 19% of the time, Pallas kernels for 0%

commit v1 on v0

--- a/solution.py
+++ b/solution.py
@@ -7,6 +7,13 @@
 STEPS = 40
 GUIDANCE = 3.5
 flow_shift = 5.0
+
+
+def trade_parts(block, name, split, join):
+    size = lax.axis_size(name)
+    pieces = jnp.stack(jnp.split(block, size, axis=split), axis=0)
+    pieces = lax.all_to_all(pieces, name, split_axis=0, concat_axis=0)
+    return jnp.concatenate(pieces, axis=join)
 
 
 def from_partner(block, axis, bit):
@@ -56,7 +63,7 @@
 def per_device(queries, keys, values, latents, gain, steps_table, flags):
     attended = attend(
         (
-            lax.all_to_all(queries[0, 0], "seq", split_axis=2, concat_axis=1, tiled=True),
+            trade_parts(queries[0, 0], "seq", 2, 1),
             lax.all_to_all(keys[0, 0], "seq", split_axis=2, concat_axis=1, tiled=True),
             lax.all_to_all(values[0, 0], "seq", split_axis=2, concat_axis=1, tiled=True),
         )

time: 161 us -> 156 us (0.969)
  waiting for transfers between devices: 70.7 us -> 66.1 us
  other arithmetic: 11.6 us -> 14.3 us
  local copies, waits for them, and re-layouts: 44.6 us -> 42.2 us
    all_to_all x1, waiting for transfers between devices: 20 us -> 16.1 us  [trade_parts(): pieces = lax.all_to_all(pieces, name, split_axis=0, concat_axis=0)]
    all_to_all x1 -> x0, local copies, waits for them, and re-layouts: 3.69 us -> none  [per_device(): lax.all_to_all(queries[0, 0], 'seq', split_axis=2, concat_axis=1, tiled=T...]
    unnamed x14 -> x21, local copies, waits for them, and re-layouts: 24.7 us -> 22.4 us
where the time goes in v1:
time: 156 us; the launch traced here: 155 us
  waiting for transfers between devices  66.1 us (42%)
  local copies, waits for them, and re-layouts  42.2 us (27%)
  starting transfers between devices  17.7 us (11%)
  other arithmetic  14.3 us (9%)
  matrix products  12.3 us (8%)
  between operations  2.19 us (1%)
    unnamed x21, local copies, waits for them, and re-layouts  22.4 us
    all_to_all x1, waiting for transfers between devices, per_device(): lax.all_to_all(keys[0, 0], 'seq', split_axis=2, concat_axis=1, tiled=True)  19.9 us
    all_to_all x1, waiting for transfers between devices, trade_parts(): pieces = lax.all_to_all(pieces, name, split_axis=0, concat_axis=0)  16.1 us
    ppermute x1, waiting for transfers between devices, from_partner(): return lax.ppermute(block, axis, route)  13.1 us
    dot_general x1, matrix products, one_block(): jnp.einsum('nhqk,nkhd->nqhd', weights, value_rows, preferred_element_type...  10.9 us
    all_to_all x1, waiting for transfers between devices, per_device(): lax.all_to_all(combine(attended[0], attended[1]), 'seq', split_axis=0, co...  9.97 us
    all_to_all x1, waiting for transfers between devices, per_device(): lax.all_to_all(values[0, 0], 'seq', split_axis=2, concat_axis=1, tiled=True)  6.94 us
    all_to_all x1, local copies, waits for them, and re-layouts, per_device(): lax.all_to_all(keys[0, 0], 'seq', split_axis=2, concat_axis=1, tiled=True)  6.07 us
  transfers between devices with their start and end apart: 5, of which 5 were waited for; matrix products, arithmetic and copies ran while one was open for 19% of the time, Pallas kernels for 0%

profile of v1, /device:TPU:0, one launch (start us, length us, event | category | flops | bytes accessed | tf_op | source)
XLA Modules:
  0.0 154.6 jit_solution(15284685113646394176)
XLA Ops:
  3.5 4.4 %all-to-all-start = ((bf16[4,2,96,1024]{3,2,1,0:T(8,128)(2,1)}), bf16[4,2,96,1024]{3,2,1,0:T(8,128)(2,1)S(1)}, u32[]{:S(2)}, u32[]{:S(2)}) async-start(bf16[4,2,96,1024]{3,2,1,0:T(8,128)(2,1)} %pad_maximum_fusion), calls=%async_computation | async-start | bytes 3145728 | tf_op jit(solution)/shard_map/all_to_all | solution.py:15
  7.9 3.9 %copy.31 = bf16[1,1,2,96,4096]{3,2,4,1,0:T(2,128)(2,1)} copy(bf16[1,1,2,96,4096]{4,3,2,1,0:T(8,128)(2,1)S(1)} %copy-done.6) | data formatting | bytes 3145728 | tf_op args[1]
  11.8 16.1 %all-to-all-done = bf16[4,2,96,1024]{3,2,1,0:T(8,128)(2,1)S(1)} async-done(((bf16[4,2,96,1024]{3,2,1,0:T(8,128)(2,1)}), bf16[4,2,96,1024]{3,2,1,0:T(8,128)(2,1)S(1)}, u32[]{:S(2)}, u32[]{:S(2)}) %all-to-all-start) | async-done | bytes 1572896 | tf_op jit(solution)/shard_map/all_to_all | solution.py:15
  29.1 3.6 %all-to-all-start.1 = ((bf16[2,96,4096]{1,0,2:T(2,128)(2,1)}), bf16[2,96,4096]{1,0,2:T(2,128)(2,1)S(1)}, u32[]{:S(2)}, u32[]{:S(2)}) async-start(bf16[2,96,4096]{1,0,2:T(2,128)(2,1)} %bitcast.56), calls=%async_computation.1 | async-start | bytes 4194304 | tf_op jit(solution)/shard_map/all_to_all | solution.py:67
  32.7 5.7 %copy.35 = bf16[1,1,2,96,4096]{3,2,4,1,0:T(2,128)(2,1)} copy(bf16[1,1,2,96,4096]{4,3,2,1,0:T(8,128)(2,1)} %param.9) | data formatting | bytes 3145728 | tf_op args[2]
  38.4 19.9 %all-to-all-done.1 = bf16[2,96,4096]{1,0,2:T(2,128)(2,1)S(1)} async-done(((bf16[2,96,4096]{1,0,2:T(2,128)(2,1)}), bf16[2,96,4096]{1,0,2:T(2,128)(2,1)S(1)}, u32[]{:S(2)}, u32[]{:S(2)}) %all-to-all-start.1) | async-done | bytes 1572896 | tf_op jit(solution)/shard_map/all_to_all | solution.py:67
  59.7 3.6 %all-to-all-start.2 = ((bf16[2,96,4096]{1,0,2:T(2,128)(2,1)}), bf16[2,96,4096]{1,0,2:T(2,128)(2,1)S(1)}, u32[]{:S(2)}, u32[]{:S(2)}) async-start(bf16[2,96,4096]{1,0,2:T(2,128)(2,1)} %bitcast.10), calls=%async_computation.2 | async-start | bytes 4194304 | tf_op jit(solution)/shard_map/all_to_all | solution.py:68
  64.9 1.6 %copy.45 = bf16[96,8,8,128]{3,2,1,0:T(8,128)(2,1)} copy(bf16[96,8,8,128]{3,1,2,0:T(8,128)(2,1)S(1)} %bitcast.61) | data formatting | bytes 3145728
  66.5 6.1 %copy.32 = bf16[2,96,4,1024]{3,1,2,0:T(8,128)(2,1)} copy(bf16[2,96,4,1024]{1,0,3,2:T(2,128)(2,1)} %bitcast.55) | data formatting | bytes 3145728 | tf_op jit(solution)/shard_map/all_to_all | solution.py:67
  72.6 2.0 %copy.46 = bf16[96,8,8,128]{3,2,1,0:T(8,128)(2,1)S(1)} copy(bf16[96,8,8,128]{3,1,2,0:T(8,128)(2,1)} %bitcast.62) | data formatting | bytes 3145728
  76.0 3.6 %copy-done = f32[2,8,384,384]{2,3,1,0:T(8,128)} copy-done((f32[2,8,384,384]{2,3,1,0:T(8,128)}, f32[2,8,384,384]{2,3,1,0:T(8,128)S(1)}, u32[]{:S(2)}) %copy-start) | copy-done | bytes 9437208
  79.6 2.4 %fusion.26 = f32[2,8,384]{2,1,0:T(8,128)S(1)} fusion(f32[2,8,384,384]{2,3,1,0:T(8,128)S(1)} %fusion.12), kind=kOutput, calls=%fused_computation.35 | output fusion | flops 9437567 | bytes 9461760 | tf_op jit(solution)/shard_map/while/body/eval_jaxpr/sub | solution.py:54
  82.0 6.9 %all-to-all-done.2 = bf16[2,96,4096]{1,0,2:T(2,128)(2,1)S(1)} async-done(((bf16[2,96,4096]{1,0,2:T(2,128)(2,1)}), bf16[2,96,4096]{1,0,2:T(2,128)(2,1)S(1)}, u32[]{:S(2)}, u32[]{:S(2)}) %all-to-all-start.2) | async-done | bytes 1572896 | tf_op jit(solution)/shard_map/all_to_all | solution.py:68
  88.9 3.7 %copy.36 = bf16[2,96,4,1024]{3,1,2,0:T(8,128)(2,1)} copy(bf16[2,96,4,1024]{1,0,3,2:T(2,128)(2,1)S(1)} %bitcast.54) | data formatting | bytes 3145728 | tf_op jit(solution)/shard_map/all_to_all | solution.py:68
  92.7 1.8 %copy.47 = bf16[96,8,8,128]{3,2,1,0:T(8,128)(2,1)S(1)} copy(bf16[96,8,8,128]{3,1,2,0:T(8,128)(2,1)} %bitcast.63) | data formatting | bytes 3145728
  94.5 10.9 %fusion.15 = bf16[2,384,8,128]{3,1,2,0:T(8,128)(2,1)} fusion(bf16[2,384,8,128]{3,2,1,0:T(8,128)(2,1)S(1)} %bitcast.65, f32[2,8,384]{2,1,0:T(8,128)S(1)} %fusion.26, f32[2,8,384,384]{2,3,1,0:T(8,128)} %copy-done), kind=kOutput, calls=%fused_computation.23 | convolution fusion | flops 616569216 | bytes 12607488 | tf_op jit(solution)/shard_map/while/body/eval_jaxpr/nhqk,nkhd->nqhd/dot_general | solution.py:55
  105.4 1.6 %slice_convert_fusion = (f32[1,384,8,128]{3,1,2,0:T(8,128)S(1)}, f32[1,384,8,128]{3,1,2,0:T(8,128)S(1)}) fusion(bf16[2,384,8,128]{3,1,2,0:T(8,128)(2,1)} %fusion.15), kind=kLoop, calls=%fused_computation.24 | loop fusion | flops 786432 | bytes 4718592 | tf_op jit(solution)/shard_map/convert_element_type | solution.py:36
  112.1 2.6 %add_convert_fusion = bf16[4,96,1024]{2,1,0:T(8,128)(2,1)} fusion(f32[4,96,1024]{2,1,0:T(8,128)S(1)} %copy-done.4, f32[4,96,1024]{2,1,0:T(8,128)} %reshape.133), kind=kLoop, calls=%fused_computation.22 | loop fusion | flops 1572864 | bytes 3932160 | tf_op jit(solution)/shard_map/convert_element_type | solution.py:36
  114.8 3.8 %all-to-all-start.3 = ((bf16[4,96,1024]{2,1,0:T(8,128)(2,1)}), bf16[4,96,1024]{2,1,0:T(8,128)(2,1)S(1)}, u32[]{:S(2)}, u32[]{:S(2)}) async-start(bf16[4,96,1024]{2,1,0:T(8,128)(2,1)} %add_convert_fusion), calls=%async_computation.3 | async-start | bytes 1572864 | tf_op jit(solution)/shard_map/all_to_all | solution.py:71
  120.0 10.0 %all-to-all-done.3 = bf16[4,96,1024]{2,1,0:T(8,128)(2,1)S(1)} async-done(((bf16[4,96,1024]{2,1,0:T(8,128)(2,1)}), bf16[4,96,1024]{2,1,0:T(8,128)(2,1)S(1)}, u32[]{:S(2)}, u32[]{:S(2)}) %all-to-all-start.3) | async-done | bytes 786464 | tf_op jit(solution)/shard_map/all_to_all | solution.py:71
  132.8 2.2 %collective-permute-start = (bf16[96,4096]{1,0:T(8,128)(2,1)}, bf16[96,4096]{1,0:T(8,128)(2,1)}, u32[]{:S(2)}, u32[]{:S(2)}) collective-permute-start(bf16[96,4096]{1,0:T(8,128)(2,1)} %fusion.9), channel_id=1, source_target_pairs={{0,16},{16,0},{1,17},{17,1},{2,18},{18,2},{3,19},{19,3},{4,20},{20... | collective-permute-start | bytes 2359304 | tf_op jit(solution)/shard_map/ppermute | solution.py:26
  137.1 2.4 %fusion.7 = bf16[1,1,96,4096]{3,2,1,0:T(8,128)(2,1)} fusion(bf16[1,1,96,4096]{3,2,1,0:T(8,128)(2,1)} %param.10, f32[1,1,96,4096]{3,2,1,0:T(8,128)S(1)} %reshape.134, f32[4096]{0:T(1024)S(1)} %bitcast.67, f32[96]{0:T(128)S(1)} %add_rsqrt_fusion, f32[]{:T(128)} %bitcast), kind=kLoop, calls=%fused_computation.13 | loop fusion | flops 2359296 | bytes 3162500 | tf_op jit(solution)/shard_map/convert_element_type | solution.py:81
  139.5 13.1 %collective-permute-done = bf16[96,4096]{1,0:T(8,128)(2,1)} collective-permute-done((bf16[96,4096]{1,0:T(8,128)(2,1)}, bf16[96,4096]{1,0:T(8,128)(2,1)}, u32[]{:S(2)}, u32[]{:S(2)}) %collective-permute-start) | collective-permute-done | bytes 786464 | tf_op jit(solution)/shard_map/ppermute | solution.py:26
  152.6 2.1 %select_bitcast_fusion = bf16[1,1,96,4096]{3,2,1,0:T(8,128)(2,1)} fusion(bf16[96,4096]{1,0:T(8,128)(2,1)} %collective-permute-done, bf16[96,4096]{1,0:T(8,128)(2,1)} %fusion.9, pred[]{:T(512)} %bitcast.16), kind=kLoop, calls=%fused_computation.26 | loop fusion | flops 393216 | bytes 2359297 | tf_op jit(solution)/shard_map/broadcast_in_dim | solution.py:85
  (31 shorter events, 18.3 us)
Async XLA Ops:
  3.5 4.4 %copy-start.6 = (bf16[1,1,2,96,4096]{4,3,2,1,0:T(8,128)(2,1)S(1)}, bf16[1,1,2,96,4096]{4,3,2,1,0:T(8,128)(2,1)}, u32[]{:S(2)}) copy-start(bf16[1,1,2,96,4096]{4,3,2,1,0:T(8,128)(2,1)} %param.8) | copy-start | bytes 4718596
  3.5 24.4 %all-to-all-start = ((bf16[4,2,96,1024]{3,2,1,0:T(8,128)(2,1)}), bf16[4,2,96,1024]{3,2,1,0:T(8,128)(2,1)S(1)}, u32[]{:S(2)}, u32[]{:S(2)}) async-start(bf16[4,2,96,1024]{3,2,1,0:T(8,128)(2,1)} %pad_maximum_fusion), calls=%async_computation | async-start | bytes 3145728 | tf_op jit(solution)/shard_map/all_to_all | solution.py:15
  28.0 1.1 copy-start.2
  29.1 29.2 %all-to-all-start.1 = ((bf16[2,96,4096]{1,0,2:T(2,128)(2,1)}), bf16[2,96,4096]{1,0,2:T(2,128)(2,1)S(1)}, u32[]{:S(2)}, u32[]{:S(2)}) async-start(bf16[2,96,4096]{1,0,2:T(2,128)(2,1)} %bitcast.56), calls=%async_computation.1 | async-start | bytes 4194304 | tf_op jit(solution)/shard_map/all_to_all | solution.py:67
  58.3 1.3 copy-start.1
  59.7 29.2 %all-to-all-start.2 = ((bf16[2,96,4096]{1,0,2:T(2,128)(2,1)}), bf16[2,96,4096]{1,0,2:T(2,128)(2,1)S(1)}, u32[]{:S(2)}, u32[]{:S(2)}) async-start(bf16[2,96,4096]{1,0,2:T(2,128)(2,1)} %bitcast.10), calls=%async_computation.2 | async-start | bytes 4194304 | tf_op jit(solution)/shard_map/all_to_all | solution.py:68
  72.6 2.0 %copy-start.3 = (bf16[96,8,8,128]{3,2,1,0:T(8,128)(2,1)S(1)}, bf16[96,8,8,128]{3,2,1,0:T(8,128)(2,1)}, u32[]{:S(2)}) copy-start(bf16[96,8,8,128]{3,2,1,0:T(8,128)(2,1)} %copy.45) | copy-start | bytes 4718596
  75.9 3.6 %copy-start = (f32[2,8,384,384]{2,3,1,0:T(8,128)}, f32[2,8,384,384]{2,3,1,0:T(8,128)S(1)}, u32[]{:S(2)}) copy-start(f32[2,8,384,384]{2,3,1,0:T(8,128)S(1)} %fusion.12) | copy-start | bytes 28311556
  110.2 1.9 %copy-start.4 = (f32[4,96,1024]{2,1,0:T(8,128)S(1)}, f32[4,96,1024]{2,1,0:T(8,128)}, u32[]{:S(2)}) copy-start(f32[4,96,1024]{2,1,0:T(8,128)} %reshape.132) | copy-start | bytes 4718596
  114.8 4.5 %copy-start.7 = (bf16[1,4096]{1,0:T(2,128)(2,1)S(1)}, bf16[1,4096]{1,0:T(2,128)(2,1)}, u32[]{:S(2)}) copy-start(bf16[1,4096]{1,0:T(2,128)(2,1)} %param.11) | copy-start | bytes 24580
  114.8 15.2 %all-to-all-start.3 = ((bf16[4,96,1024]{2,1,0:T(8,128)(2,1)}), bf16[4,96,1024]{2,1,0:T(8,128)(2,1)S(1)}, u32[]{:S(2)}, u32[]{:S(2)}) async-start(bf16[4,96,1024]{2,1,0:T(8,128)(2,1)} %add_convert_fusion), calls=%async_computation.3 | async-start | bytes 1572864 | tf_op jit(solution)/shard_map/all_to_all | solution.py:71
  130.4 1.1 copy-start.5
  132.8 19.8 %collective-permute-start = (bf16[96,4096]{1,0:T(8,128)(2,1)}, bf16[96,4096]{1,0:T(8,128)(2,1)}, u32[]{:S(2)}, u32[]{:S(2)}) collective-permute-start(bf16[96,4096]{1,0:T(8,128)(2,1)} %fusion.9), channel_id=1, source_target_pairs={{0,16},{16,0},{1,17},{17,1},{2,18},{18,2},{3,19},{19,3},{4,20},{20... | collective-permute-start | bytes 2359304 | tf_op jit(solution)/shard_map/ppermute | solution.py:26
